TPU v7x, 32 devices: a whole 2x2x4 slice. The times are simulated.
32 devices in a mesh: dp: 16 (over z, y, core), local: 2 (over x).
Axes of the slice: x: 2, y: 2, z: 4, core: 2. Of those that a mesh axis runs over, the one named last changes fastest.
Arguments:
- pre_glu: bfloat16 [32, 256, 3072], P(('dp', 'local')), may hold values from -80 to 80
- lengths: int32 [32], P(('dp', 'local')), may hold values from 1 to 256, as said below
- kernel: float32 [5, 1536], replicated, may hold values from -2.5 to 2.5
- bn_gain: float32 [1536], replicated, may hold values from 0.5 to 2
- bn_shift: float32 [1536], replicated, may hold values from -1 to 1
- w_out: bfloat16 [1536, 1536], replicated, may hold values from -0.15625 to 0.15625
- cotangent: bfloat16 [32, 256, 1536], P(('dp', 'local')), may hold values from -6 to 6
Outputs:
- grad_pre_glu: bfloat16 [32, 256, 3072], P(('dp', 'local'))
- grad_w_out: float32 [1536, 1536], P('dp', 'local')
- grad_kernel: float32 [5, 1536], replicated
- grad_gain: float32 [1536], replicated
- grad_shift: float32 [1536], replicated
Inputs may be any that keep to these rules, and one draw needn't show every extreme that they name: `lengths`: each utterance's valid frames are its first ones; some utterance has all 256 frames valid.
All inputs are finite; a program needn't handle non-finite values.
Results may differ from a plain program's by a relative error of at most 0.0029.
Values sent between devices are 32-bit elements; how exact they have to be, the bound alone decides.
A program may use at most 64 MiB of HBM per device.

v0:
```python
import jax
import jax.numpy as jnp
from jax import lax
from jax.sharding import PartitionSpec as P

epsilon = 1e-05


def on_device(pre_glu, lengths, kernel, bn_gain, bn_shift, w_out, cotangent):
    frames = pre_glu.shape[1]
    model_width = kernel.shape[1]
    kernel_taps = kernel.shape[0]
    half_width = (kernel_taps - 1) // 2
    replicas = lax.axis_size("dp") * lax.axis_size("local")
    valid_mask = (jnp.arange(frames, dtype=jnp.int32)[:, None] < lengths[0]).astype(jnp.float32)
    first_half = pre_glu[0, :, :model_width].astype(jnp.float32)
    gate_value = jax.nn.sigmoid(pre_glu[0, :, model_width:].astype(jnp.float32))
    glu_out = first_half * gate_value * valid_mask
    padded = jnp.pad(glu_out, ((half_width, half_width), (0, 0)))
    conv_out = kernel[0] * padded[0:frames]
    for j in range(1, kernel_taps):
        conv_out = conv_out + kernel[j] * padded[j : j + frames]
    own_count = lengths[0].astype(jnp.float32)
    sum_first, sum_square, frame_total = lax.psum(
        (
            jnp.sum(conv_out * valid_mask, 0),
            jnp.sum(conv_out * conv_out * valid_mask, 0),
            own_count,
        ),
        ("dp", "local"),
    )
    mean_value = sum_first / frame_total
    variance = sum_square / frame_total - mean_value * mean_value
    invstd = lax.rsqrt(variance + epsilon)
    normed = (conv_out - mean_value) * invstd
    act_in = bn_gain * normed + bn_shift
    sig_act = jax.nn.sigmoid(act_in)
    swished = (act_in * sig_act).astype(jnp.bfloat16)
    masked_cot = cotangent[0] * valid_mask.astype(jnp.bfloat16)
    contract = (((0,), (0,)), ((), ()))
    wgrad_term = lax.dot_general(swished, masked_cot, contract, preferred_element_type=jnp.float32)
    partial_value = lax.psum_scatter(wgrad_term, "dp", scatter_dimension=0, tiled=True)
    weight_shard = lax.psum_scatter(partial_value, "local", scatter_dimension=1, tiled=True)
    grad_swish = lax.dot_general(
        masked_cot, w_out, (((1,), (1,)), ((), ())), preferred_element_type=jnp.float32
    )
    grad_act = grad_swish * sig_act * (1.0 + act_in * (1.0 - sig_act))
    channel_scale = bn_gain * invstd
    sum_shift, sum_gain = lax.psum(
        (jnp.sum(grad_act, 0), jnp.sum(grad_act * normed, 0)), ("dp", "local")
    )
    grad_conv = (
        valid_mask * channel_scale * (grad_act - (sum_shift + normed * sum_gain) / frame_total)
    )
    kernel_part = jnp.stack(
        [jnp.sum(grad_conv * padded[j : j + frames], 0) for j in range(kernel_taps)], 0
    )
    kernel_sum = lax.psum(kernel_part, ("dp", "local"))
    grad_padded = jnp.pad(grad_conv, ((half_width, half_width), (0, 0)))
    grad_glu = kernel[0] * grad_padded[kernel_taps - 1 : kernel_taps - 1 + frames]
    for j in range(1, kernel_taps):
        grad_glu = (
            grad_glu + kernel[j] * grad_padded[kernel_taps - 1 - j : kernel_taps - 1 - j + frames]
        )
    grad_glu = grad_glu * valid_mask
    grad_first = grad_glu * gate_value
    grad_second = grad_glu * first_half * gate_value * (1.0 - gate_value)
    grad_pre = jnp.concatenate([grad_first, grad_second], 1).astype(jnp.bfloat16)[None]
    return (
        grad_pre,
        weight_shard / replicas,
        kernel_sum / replicas,
        sum_gain / replicas,
        sum_shift / replicas,
    )


def solution(mesh):
    return jax.shard_map(
        on_device,
        mesh=mesh,
        in_specs=(
            P(("dp", "local"), None, None),
            P(("dp", "local")),
            P(),
            P(),
            P(),
            P(),
            P(("dp", "local"), None, None),
        ),
        out_specs=(P(("dp", "local"), None, None), P("dp", "local"), P(), P(), P()),
        check_vma=False,
    )
```

profile of v0, /device:TPU:0, one launch (start us, length us, event | category | flops | bytes accessed | tf_op | source)
XLA Modules:
  0.0 228.4 jit_solution(6184416316779539486)
XLA Ops:
  7.2 0.0 reduce-scatter.3.cloned.1.call-start
  7.9 1.1 slice_reduce_fusion.4
  9.0 1.8 fusion.1
  10.8 0.0 copy-start.2
  10.8 0.0 copy-start.3
  10.8 1.1 multiply_reduce_fusion.7
  11.9 42.4 %all-reduce.3 = (f32[1536]{0:T(1024)S(1)}, f32[]{:T(128)}, f32[1536]{0:T(1024)S(1)}) all-reduce(f32[1536]{0:T(1024)S(1)} %get-tuple-element.11, f32[]{:T(128)S(6)} %convert_element_type.50, f32[1536]{0:T(1024)S(1)} %get-tuple-element.10), channel_id=1, replica_groups=mesh['dp'=16,'local'=2] {'dp','local'}, use_global_device_ids=true, to_apply=%region_4.5 | all-reduce | flops 3073 | bytes 24584 | tf_op jit(solution)/shard_map/psum | solution.py:24
  54.4 0.0 copy-done.2
  54.4 0.7 fusion.17
  55.0 0.7 add_rsqrt_fusion
  55.7 0.0 copy-done.3
  55.7 6.4 %fusion.7 = f32[1536,1536]{1,0:T(8,128)} fusion(f32[256,1536]{1,0:T(8,128)S(1)} %get-tuple-element.29, f32[1536]{0:T(1024)S(1)} %copy-done.3, f32[1536]{0:T(1024)S(1)} %add_rsqrt_fusion, f32[1536]{0:T(1024)S(1)} %get-tuple-element.28, f32[1536]{0:T(1024)S(1)} %copy-done.2, bf16[1,256,1536]{2,1,0:T(8,128)(2,1)} %param.13, bf16[256]{0:T(256)(128)(2,1)S(1)} %fusion.18), kind=kOutput, calls=%fused_computation.33 | convolution fusion | flops 1211891712 | bytes 11821568 | tf_op jit(solution)/shard_map/dot_general | solution.py:41
  62.1 0.0 reduce-scatter.3.cloned.1.call-update
  62.2 0.0 reduce-scatter.5.cloned.1.call-start
  62.2 5.6 %fusion.20 = (f32[1536]{0:T(1024)S(1)}, f32[1536]{0:T(1024)S(1)}, f32[256,1536]{1,0:T(8,128)}) fusion(f32[1536]{0:T(1024)S(1)} %add_rsqrt_fusion, f32[256,1536]{1,0:T(8,128)S(1)} %get-tuple-element.29, f32[1536]{0:T(1024)S(1)} %get-tuple-element.28, f32[1536]{0:T(1024)S(1)} %copy-done.3, f32[1536]{0:T(1024)S(1)} %copy-done.2, ...), kind=kOutput, calls=%fused_computation.60 | convolution fusion | flops 1214247936 | bytes 8688128 | tf_op jit(solution)/shard_map/dot_general | solution.py:44
  67.8 41.1 %all-reduce.2 = (f32[1536]{0:T(1024)S(1)}, f32[1536]{0:T(1024)S(1)}) all-reduce(f32[1536]{0:T(1024)S(1)} %get-tuple-element.13, f32[1536]{0:T(1024)S(1)} %get-tuple-element.12), channel_id=1, replica_groups=mesh['dp'=16,'local'=2] {'dp','local'}, use_global_device_ids=true, to_apply=%region_8.9 | all-reduce | flops 3072 | bytes 24576 | tf_op jit(solution)/shard_map/psum | solution.py:49
  108.9 0.0 copy-start
  108.9 3.5 %multiply_reduce_fusion = (f32[1536]{0:T(1024)S(1)}, f32[1536]{0:T(1024)S(1)}, f32[1536]{0:T(1024)S(1)}, f32[1536]{0:T(1024)S(1)}, f32[1536]{0:T(1024)S(1)}, /*index=5*/f32[256,1536]{1,0:T(8,128)S(1)}) fusion(f32[256,1536]{1,0:T(8,128)S(1)} %fusion.1, f32[256,1536]{1,0:T(8,128)} %get-tuple-element.30, f32[]{:T(128)} %get-tuple-element.22, ...), kind=kLoop, calls=%fused_computation.12 | loop fusion | flops 7070208 | bytes 6353924 | tf_op jit(solution)/shard_map/reduce_sum | solution.py:56
  112.4 0.0 copy-done
  112.4 0.0 copy-start.1
  112.4 2.2 fusion.8
  114.6 59.1 %reduce-scatter.3.cloned.1.call-done = f32[96,1536]{1,0:T(8,128)} async-done(((f32[1536,1536]{1,0:T(8,128)}), f32[96,1536]{1,0:T(8,128)}) %reduce-scatter.3.cloned.1.call-update) | async-done | bytes 589840 | tf_op jit(solution)/shard_map/reduce_scatter | solution.py:42
  173.7 0.0 reduce-scatter.5.cloned.1.call-update
  173.7 0.0 copy-done.1
  173.7 1.4 fusion.9
  175.2 0.1 stack.23
  175.2 40.7 %psum.47 = f32[5,1536]{1,0:T(8,128)S(1)} all-reduce(f32[5,1536]{1,0:T(8,128)S(1)} %stack.23), channel_id=1, replica_groups=mesh['dp'=16,'local'=2] {'dp','local'}, use_global_device_ids=true, to_apply=%region_16.17 | all-reduce | flops 7680 | bytes 61440 | tf_op jit(solution)/shard_map/psum | solution.py:58
  216.0 0.6 broadcast_multiply_fusion.2
  216.6 2.7 %pad_maximum_fusion = bf16[1,256,3072]{2,1,0:T(8,128)(2,1)} fusion(bf16[1,256,1536]{2,1,0:T(8,128)(2,1)} %fusion.9, bf16[1,256,1536]{2,1,0:T(8,128)(2,1)} %get-tuple-element.25), kind=kLoop, calls=%fused_computation.8 | loop fusion | flops 3145728 | bytes 3145728 | tf_op jit(solution)/shard_map/concatenate | solution.py:68
  219.2 0.6 broadcast_multiply_fusion.1
  219.9 0.0 reduce-scatter.5.cloned.1.call-done
  219.9 1.7 broadcast_multiply_fusion
  (7 shorter events, 0.0 us)
Async XLA Ops:
  7.2 166.5 %reduce-scatter.3.cloned.1.call-start = ((), (), s32[]{:S(2)}) async-start(), calls=%async_computation.2 | async-start | bytes 10027008 | tf_op jit(solution)/shard_map/reduce_scatter | solution.py:42
  10.8 43.6 %copy-start.2 = (f32[1536]{0:T(1024)S(1)}, f32[1536]{0:T(1024)}, u32[]{:S(2)}) copy-start(f32[1536]{0:T(1024)} %param.10) | copy-start | bytes 18436
  10.8 44.9 %copy-start.3 = (f32[1536]{0:T(1024)S(1)}, f32[1536]{0:T(1024)}, u32[]{:S(2)}) copy-start(f32[1536]{0:T(1024)} %param.11) | copy-start | bytes 18436
  62.2 157.7 %reduce-scatter.5.cloned.1.call-start = ((), (), s32[]{:S(2)}) async-start(), calls=%async_computation.3 | async-start | bytes 884736 | tf_op jit(solution)/shard_map/reduce_scatter | solution.py:43
  108.9 3.5 %copy-start = (bf16[1,256,3072]{2,1,0:T(8,128)(2,1)S(1)}, bf16[1,256,3072]{2,1,0:T(8,128)(2,1)}, u32[]{:S(2)}) copy-start(bf16[1,256,3072]{2,1,0:T(8,128)(2,1)} %param.7) | copy-start | bytes 4718596
  112.4 61.3 %copy-start.1 = (bf16[1,256,3072]{2,1,0:T(8,128)(2,1)S(1)}, bf16[1,256,3072]{2,1,0:T(8,128)(2,1)}, u32[]{:S(2)}) copy-start(bf16[1,256,3072]{2,1,0:T(8,128)(2,1)} %param.7) | copy-start | bytes 4718596
Sparse Core Ops, SparseCore 0:
  62.3 111.3 reduce-scatter.2
  175.9 15.2 reduce-scatter.4
where the time goes:
time: 229 us; the launch traced here: 228 us
  blocking collectives  124 us (54%)
  waiting for transfers between devices  59.1 us (26%)
  other arithmetic  16.9 us (7%)
  between operations  14.8 us (6%)
  matrix products  12 us (5%)
    reduce_scatter x1, waiting for transfers between devices, on_device(): lax.psum_scatter(wgrad_term, 'dp', scatter_dimension=0, tiled=True)  59.1 us
    psum x1, blocking collectives, on_device(): lax.psum((jnp.sum(conv_out * valid_mask, 0), jnp.sum(conv_out * conv_out...  42.4 us
    psum x1, blocking collectives, on_device(): lax.psum((jnp.sum(grad_act, 0), jnp.sum(grad_act * normed, 0)), ('dp', 'l...  41.1 us
    psum x1, blocking collectives, on_device(): kernel_sum = lax.psum(kernel_part, ('dp', 'local'))  40.7 us
    dot_general x1, matrix products, on_device(): lax.dot_general(swished, masked_cot, contract, preferred_element_type=jnp...  6.43 us
    concatenate x3, other arithmetic, on_device(): jnp.concatenate([grad_first, grad_second], 1).astype(jnp.bfloat16)[None]  6.24 us
    dot_general x1, matrix products, on_device(): lax.dot_general(masked_cot, w_out, (((1,), (1,)), ((), ())), preferred_el...  5.56 us
  transfers between devices with their start and end apart: 2, of which 1 were waited for; matrix products, arithmetic and copies ran while one was open for 7% of the time, Pallas kernels for 0%

commit v1 on v0

--- a/solution.py
+++ b/solution.py
@@ -4,6 +4,11 @@
 from jax.sharding import PartitionSpec as P
 
 epsilon = 1e-05
+
+
+def gather_and_add(x, mesh_axis):
+    blocks = lax.all_gather(x, mesh_axis)
+    return jnp.sum(blocks, axis=0)
 
 
 def on_device(pre_glu, lengths, kernel, bn_gain, bn_shift, w_out, cotangent):
@@ -55,7 +60,7 @@
     kernel_part = jnp.stack(
         [jnp.sum(grad_conv * padded[j : j + frames], 0) for j in range(kernel_taps)], 0
     )
-    kernel_sum = lax.psum(kernel_part, ("dp", "local"))
+    kernel_sum = gather_and_add(kernel_part, ("dp", "local"))
     grad_padded = jnp.pad(grad_conv, ((half_width, half_width), (0, 0)))
     grad_glu = kernel[0] * grad_padded[kernel_taps - 1 : kernel_taps - 1 + frames]
     for j in range(1, kernel_taps):

time: 229 us -> 261 us (1.14)
  blocking collectives: 124 us -> 159 us
  waiting for transfers between devices: 59.1 us -> 54.4 us
    all_gather x0 -> x1, blocking collectives: none -> 75.7 us  [gather_and_add(): blocks = lax.all_gather(x, mesh_axis)]
    psum x1 -> x0, blocking collectives: 40.7 us -> none  [on_device(): kernel_sum = lax.psum(kernel_part, ('dp', 'local'))]
    reduce_scatter x1, waiting for transfers between devices: 59.1 us -> 54.4 us  [on_device(): lax.psum_scatter(wgrad_term, 'dp', scatter_dimension=0, tiled=True)]
where the time goes in v1:
time: 261 us
  blocking collectives  159 us (61%)
  waiting for transfers between devices  54.4 us (21%)
  other arithmetic  18.9 us (7%)
  between operations  14.8 us (6%)
  matrix products  12 us (5%)
    all_gather x1, blocking collectives, gather_and_add(): blocks = lax.all_gather(x, mesh_axis)  75.7 us
    reduce_scatter x1, waiting for transfers between devices, on_device(): lax.psum_scatter(wgrad_term, 'dp', scatter_dimension=0, tiled=True)  54.4 us
    psum x1, blocking collectives, on_device(): lax.psum((jnp.sum(conv_out * valid_mask, 0), jnp.sum(conv_out * conv_out...  42.4 us
    psum x1, blocking collectives, on_device(): lax.psum((jnp.sum(grad_act, 0), jnp.sum(grad_act * normed, 0)), ('dp', 'l...  41.1 us
    concatenate x3, other arithmetic, on_device(): jnp.concatenate([grad_first, grad_second], 1).astype(jnp.bfloat16)[None]  7.43 us
    dot_general x1, matrix products, on_device(): lax.dot_general(swished, masked_cot, contract, preferred_element_type=jnp...  6.43 us
    dot_general x1, matrix products, on_device(): lax.dot_general(masked_cot, w_out, (((1,), (1,)), ((), ())), preferred_el...  5.56 us
  transfers between devices with their start and end apart: 2, of which 1 were waited for; matrix products, arithmetic and copies ran while one was open for 7% of the time, Pallas kernels for 0%

profile of v1, /device:TPU:0, one launch (start us, length us, event | category | flops | bytes accessed | tf_op | source)
XLA Modules:
  0.0 260.6 jit_solution(2931396110375079881)
XLA Ops:
  7.2 0.0 reduce-scatter.3.cloned.1.call-start
  7.9 1.1 slice_reduce_fusion.4
  9.0 1.8 fusion.1
  10.8 0.0 copy-start.1
  10.8 0.0 copy-start.2
  10.8 1.1 multiply_reduce_fusion.7
  11.9 42.4 %all-reduce.3 = (f32[1536]{0:T(1024)S(1)}, f32[]{:T(128)}, f32[1536]{0:T(1024)S(1)}) all-reduce(f32[1536]{0:T(1024)S(1)} %get-tuple-element.11, f32[]{:T(128)S(6)} %convert_element_type.50, f32[1536]{0:T(1024)S(1)} %get-tuple-element.10), channel_id=1, replica_groups=mesh['dp'=16,'local'=2] {'dp','local'}, use_global_device_ids=true, to_apply=%region_4.5 | all-reduce | flops 3073 | bytes 24584 | tf_op jit(solution)/shard_map/psum | solution.py:29
  54.4 0.0 copy-done.1
  54.4 0.7 fusion.17
  55.0 0.7 add_rsqrt_fusion
  55.7 0.0 copy-done.2
  55.7 6.4 %fusion.7 = f32[1536,1536]{1,0:T(8,128)} fusion(f32[256,1536]{1,0:T(8,128)S(1)} %get-tuple-element.29, f32[1536]{0:T(1024)S(1)} %copy-done.2, f32[1536]{0:T(1024)S(1)} %add_rsqrt_fusion, f32[1536]{0:T(1024)S(1)} %get-tuple-element.28, f32[1536]{0:T(1024)S(1)} %copy-done.1, bf16[1,256,1536]{2,1,0:T(8,128)(2,1)} %param.13, bf16[256]{0:T(256)(128)(2,1)S(1)} %fusion.18), kind=kOutput, calls=%fused_computation.33 | convolution fusion | flops 1211891712 | bytes 11821568 | tf_op jit(solution)/shard_map/dot_general | solution.py:46
  62.1 0.0 reduce-scatter.3.cloned.1.call-update
  62.2 0.0 reduce-scatter.5.cloned.1.call-start
  62.2 5.6 %fusion.20 = (f32[1536]{0:T(1024)S(1)}, f32[1536]{0:T(1024)S(1)}, f32[256,1536]{1,0:T(8,128)}) fusion(f32[1536]{0:T(1024)S(1)} %add_rsqrt_fusion, f32[256,1536]{1,0:T(8,128)S(1)} %get-tuple-element.29, f32[1536]{0:T(1024)S(1)} %get-tuple-element.28, f32[1536]{0:T(1024)S(1)} %copy-done.2, f32[1536]{0:T(1024)S(1)} %copy-done.1, ...), kind=kOutput, calls=%fused_computation.60 | convolution fusion | flops 1214247936 | bytes 8688128 | tf_op jit(solution)/shard_map/dot_general | solution.py:49
  67.8 41.1 %all-reduce.2 = (f32[1536]{0:T(1024)S(1)}, f32[1536]{0:T(1024)S(1)}) all-reduce(f32[1536]{0:T(1024)S(1)} %get-tuple-element.13, f32[1536]{0:T(1024)S(1)} %get-tuple-element.12), channel_id=1, replica_groups=mesh['dp'=16,'local'=2] {'dp','local'}, use_global_device_ids=true, to_apply=%region_8.9 | all-reduce | flops 3072 | bytes 24576 | tf_op jit(solution)/shard_map/psum | solution.py:54
  108.9 4.2 %multiply_reduce_fusion = (f32[1536]{0:T(1024)S(1)}, f32[1536]{0:T(1024)S(1)}, f32[1536]{0:T(1024)S(1)}, f32[1536]{0:T(1024)S(1)}, f32[1536]{0:T(1024)S(1)}, /*index=5*/f32[256,1536]{1,0:T(8,128)}) fusion(f32[256,1536]{1,0:T(8,128)S(1)} %fusion.1, f32[256,1536]{1,0:T(8,128)} %get-tuple-element.30, f32[]{:T(128)} %get-tuple-element.22, ...), kind=kLoop, calls=%fused_computation.12 | loop fusion | flops 7070208 | bytes 6353924 | tf_op jit(solution)/shard_map/reduce_sum | solution.py:61
  113.1 0.1 stack.23
  113.2 0.0 copy-start
  113.2 5.5 %fusion.8 = (bf16[1,256,1536]{2,1,0:T(8,128)(2,1)S(1)}, f32[256,1536]{1,0:T(8,128)S(1)}) fusion(bf16[1,256,3072]{2,1,0:T(8,128)(2,1)} %param.7, f32[256]{0:T(256)S(1)} %compare_convert_fusion, f32[1536]{0:T(1024)S(1)} %get-tuple-element.17, f32[1536]{0:T(1024)S(1)} %get-tuple-element.18, f32[256,1536]{1,0:T(8,128)} %get-tuple-element.24, ...), kind=kLoop, calls=%fused_computation.34 | loop fusion | flops 6291456 | bytes 4750336 | tf_op jit(solution)/shard_map/concatenate | solution.py:73
  118.7 0.0 copy-done
  118.7 0.5 fusion.9
  119.3 54.4 %reduce-scatter.3.cloned.1.call-done = f32[96,1536]{1,0:T(8,128)} async-done(((f32[1536,1536]{1,0:T(8,128)}), f32[96,1536]{1,0:T(8,128)}) %reduce-scatter.3.cloned.1.call-update) | async-done | bytes 589840 | tf_op jit(solution)/shard_map/reduce_scatter | solution.py:47
  173.7 0.0 reduce-scatter.5.cloned.1.call-update
  173.7 75.7 %all-gather.1 = f32[32,5,1536]{2,1,0:T(8,128)S(1)} all-gather(f32[1,5,1536]{2,1,0:T(8,128)S(1)} %bitcast.33), channel_id=2, replica_groups=mesh['dp'=16,'local'=2] {'dp','local'}, dimensions={0}, use_global_device_ids=true | all-gather | bytes 1013760 | tf_op jit(solution)/shard_map/all_gather | solution.py:10
  249.4 0.1 reduce_sum.99
  249.5 0.6 broadcast_multiply_fusion.2
  250.1 1.4 pad_maximum_fusion
  251.5 0.6 broadcast_multiply_fusion.1
  252.1 0.0 reduce-scatter.5.cloned.1.call-done
  252.1 1.7 broadcast_multiply_fusion
  (7 shorter events, 0.0 us)
Async XLA Ops:
  7.2 166.5 %reduce-scatter.3.cloned.1.call-start = ((), (), s32[]{:S(2)}) async-start(), calls=%async_computation.2 | async-start | bytes 10027008 | tf_op jit(solution)/shard_map/reduce_scatter | solution.py:47
  10.8 43.6 %copy-start.1 = (f32[1536]{0:T(1024)S(1)}, f32[1536]{0:T(1024)}, u32[]{:S(2)}) copy-start(f32[1536]{0:T(1024)} %param.10) | copy-start | bytes 18436
  10.8 44.9 %copy-start.2 = (f32[1536]{0:T(1024)S(1)}, f32[1536]{0:T(1024)}, u32[]{:S(2)}) copy-start(f32[1536]{0:T(1024)} %param.11) | copy-start | bytes 18436
  62.2 189.9 %reduce-scatter.5.cloned.1.call-start = ((), (), s32[]{:S(2)}) async-start(), calls=%async_computation.3 | async-start | bytes 884736 | tf_op jit(solution)/shard_map/reduce_scatter | solution.py:48
  113.2 5.5 %copy-start = (bf16[1,256,3072]{2,1,0:T(8,128)(2,1)S(1)}, bf16[1,256,3072]{2,1,0:T(8,128)(2,1)}, u32[]{:S(2)}) copy-start(bf16[1,256,3072]{2,1,0:T(8,128)(2,1)} %param.7) | copy-start | bytes 4718596
Sparse Core Ops, SparseCore 0:
  62.3 111.3 reduce-scatter.2
  175.9 18.5 reduce-scatter.4
